TPU v7x, 32 devices: a whole 2x2x4 slice. The times are simulated.
32 devices in a mesh: dp: 2 (over x), tp: 4 (over z), section: 4 (over y, core).
Axes of the slice: x: 2, y: 2, z: 4, core: 2. Of those that a mesh axis runs over, the one named last changes fastest.
Arguments:
- tokens: bfloat16 [256, 2304], P('dp', 'section'), may hold values from -6 to 6
- hidden_grad: bfloat16 [256, 18432], P('dp', ('tp', 'section')), may hold values from -6 to 6
- norm_gain: float32 [2304], replicated, may hold values from 0.5 to 1.5
- w_gate: bfloat16 [2304, 18432], P('dp', ('tp', 'section')), may hold values from -0.125 to 0.125
- w_up: bfloat16 [2304, 18432], P('dp', ('tp', 'section')), may hold values from -0.125 to 0.125
Outputs:
- grad_tokens: bfloat16 [256, 2304], P('dp', ('tp', 'section'))
- grad_gain: float32 [2304], P(('tp', 'section'))
- grad_gate: bfloat16 [2304, 18432], P('dp', ('tp', 'section'))
- grad_up: bfloat16 [2304, 18432], P('dp', ('tp', 'section'))
All inputs are finite; a program needn't handle non-finite values.
Results may differ from a plain program's by a relative error of at most 0.018.
Values may be sent and summed in bfloat16 or wider, within the bound.
A program may use at most 128 MiB of HBM per device.

v0:
```python
import jax
import jax.numpy as jnp
from jax import lax
from jax.sharding import PartitionSpec as P

D = 2304
epsilon = 1e-06


def gated_unit(gate, up):
    return jax.nn.gelu(gate, approximate=True) * up


def shards(tokens, hidden_grad, norm_gain, w_gate, w_up):
    rows_in = lax.all_gather(tokens, "section", axis=1, tiled=True)
    inputs = rows_in.astype(jnp.float32)
    inv_rms = lax.rsqrt(jnp.mean(inputs * inputs, axis=1) + epsilon)
    normed = (inputs * inv_rms[:, None] * norm_gain).astype(jnp.bfloat16)
    full_gate, full_up = (
        lax.all_gather(w_gate, "dp", axis=0, tiled=True),
        lax.all_gather(w_up, "dp", axis=0, tiled=True),
    )
    gate = jnp.dot(normed, full_gate, preferred_element_type=jnp.float32)
    up = jnp.dot(normed, full_up, preferred_element_type=jnp.float32)
    hidden, pull = jax.vjp(gated_unit, gate, up)
    d_gate, d_up = pull(hidden_grad.astype(jnp.float32))
    d_gate = d_gate.astype(jnp.bfloat16)
    d_up = d_up.astype(jnp.bfloat16)
    contract_cols = (((1,), (1,)), ((), ()))
    contract_rows = (((0,), (0,)), ((), ()))
    features = full_gate.shape[0]
    own_width = features // lax.axis_size(("tp", "section"))
    first = lax.dot_general(full_gate, d_gate, contract_cols, preferred_element_type=jnp.float32)
    second = lax.dot_general(full_up, d_up, contract_cols, preferred_element_type=jnp.float32)
    d_columns = lax.psum_scatter(
        (first + second).astype(jnp.bfloat16), ("tp", "section"), scatter_dimension=0, tiled=True
    ).astype(jnp.float32)
    d_normed = d_columns.T
    offset = lax.axis_index(("tp", "section")) * own_width
    own_inputs = lax.dynamic_slice_in_dim(inputs, offset, own_width, 1)
    own_gain = lax.dynamic_slice_in_dim(norm_gain, offset, own_width, 0)
    gain_part = jnp.sum(d_normed * own_inputs * inv_rms[:, None], axis=0)
    row_part = jnp.sum(own_inputs * own_gain * d_normed, axis=1)
    grad_gain = lax.psum(gain_part, "dp")
    row_sum = lax.psum(row_part, ("tp", "section"))
    grad_tokens = (
        inv_rms[:, None] * own_gain * d_normed - own_inputs * (inv_rms**3 * row_sum / D)[:, None]
    )
    block = w_gate.shape[0]
    fwidth = w_gate.shape[1]
    cols_normed = lax.all_to_all(normed, "dp", split_axis=1, concat_axis=0, tiled=True)
    per_device = normed.shape[0]
    empty = jnp.zeros((block, fwidth), jnp.float32)
    piece_gate = lax.all_gather(d_gate, "dp", axis=0, tiled=True)
    piece_up = lax.all_gather(d_up, "dp", axis=0, tiled=True)

    def one_block(index, running):
        inner = index * per_device
        block_normed = lax.dynamic_slice_in_dim(cols_normed, inner, per_device, 0)
        block_gate = lax.dynamic_slice_in_dim(piece_gate, inner, per_device, 0)
        block_up = lax.dynamic_slice_in_dim(piece_up, inner, per_device, 0)
        terms = (
            lax.dot_general(
                block_normed, block_gate, contract_rows, preferred_element_type=jnp.float32
            ),
            lax.dot_general(
                block_normed, block_up, contract_rows, preferred_element_type=jnp.float32
            ),
        )
        return tuple(
            (
                total + lax.optimization_barrier(term.astype(jnp.bfloat16)).astype(jnp.float32)
                for total, term in zip(running, terms)
            )
        )

    sum_gate, sum_up = lax.fori_loop(
        0, piece_gate.shape[0] // per_device, one_block, (empty, empty)
    )
    return (
        grad_tokens.astype(jnp.bfloat16),
        grad_gain,
        sum_gate.astype(jnp.bfloat16),
        sum_up.astype(jnp.bfloat16),
    )


def solution(mesh):
    in_specs = (
        P("dp", "section"),
        P("dp", ("tp", "section")),
        P(),
        P("dp", ("tp", "section")),
        P("dp", ("tp", "section")),
    )
    out_specs = (
        P("dp", ("tp", "section")),
        P(("tp", "section")),
        P("dp", ("tp", "section")),
        P("dp", ("tp", "section")),
    )
    return jax.shard_map(shards, mesh=mesh, in_specs=in_specs, out_specs=out_specs, check_vma=False)
```

profile of v0, /device:TPU:0, one launch (start us, length us, event | category | flops | bytes accessed | tf_op | source)
XLA Modules:
  0.0 266.3 jit_solution(6498756828406113752)
XLA Ops:
  7.2 0.0 copy-start.3
  7.2 0.0 copy-start.4
  7.2 0.0 all-gather.5.cloned.1.call-start
  7.2 0.7 all-gather.5.cloned.1.call-update
  7.9 0.0 copy-start.2
  7.9 0.0 all-gather.3.cloned.1.call-start
  8.0 0.7 all-gather.3.cloned.1.call-update
  8.7 0.0 copy-done.3
  8.7 9.0 %all_gather.15 = bf16[128,2304]{0,1:T(8,128)(2,1)S(1)} all-gather(bf16[128,576]{0,1:T(8,128)(2,1)S(1)} %copy-done.3), channel_id=1, replica_groups=mesh['dp'=2,'tp'=4,'section'=4] {'section'}, dimensions={1}, use_global_device_ids=true | all-gather | bytes 737280 | tf_op jit(solution)/shard_map/all_gather | solution.py:15
  17.7 0.3 multiply_reduce_fusion
  18.1 0.0 copy-done.4
  18.1 0.4 multiply_convert_fusion
  18.4 1.1 copy.13
  19.5 3.5 %all-to-all-start = ((bf16[128,2,1152]{2,0,1:T(8,128)(2,1)}), bf16[128,2,1152]{2,0,1:T(8,128)(2,1)S(1)}, u32[]{:S(2)}, u32[]{:S(2)}) async-start(bf16[128,2,1152]{2,0,1:T(8,128)(2,1)} %copy.13), calls=%async_computation | async-start | bytes 1179648 | tf_op jit(solution)/shard_map/all_to_all | solution.py:51
  23.0 0.0 reduce-scatter.4.cloned.1.call-start
  23.1 1.1 convert_element_type.59
  24.2 0.1 dynamic_slice.27
  24.3 63.6 %all-gather.5.cloned.1.call-done = bf16[2304,1152]{1,0:T(8,128)(2,1)} async-done(((bf16[1152,1152]{1,0:T(8,128)(2,1)}), bf16[2304,1152]{1,0:T(8,128)(2,1)}) %all-gather.5.cloned.1.call-update) | async-done | bytes 5308432 | tf_op jit(solution)/shard_map/all_gather | solution.py:20
  87.9 0.0 copy-done.2
  87.9 0.0 slice-start
  87.9 3.7 %fusion.8 = (bf16[128,1152]{1,0:T(8,128)(2,1)S(1)}, f32[128,1152]{1,0:T(8,128)S(1)}) fusion(bf16[128,1152]{1,0:T(8,128)(2,1)S(1)} %copy-done.2, bf16[128,2304]{0,1:T(8,128)(2,1)S(1)} %multiply_convert_fusion, bf16[2304,1152]{1,0:T(8,128)(2,1)} %all-gather.5.cloned.1.call-done), kind=kOutput, calls=%fused_computation.19 | convolution fusion | flops 681099264 | bytes 7077888 | tf_op jit(solution)/shard_map/dot_general | solution.py:23
  91.6 67.1 %all-gather.3.cloned.1.call-done = bf16[2304,1152]{1,0:T(8,128)(2,1)} async-done(((bf16[1152,1152]{1,0:T(8,128)(2,1)}), bf16[2304,1152]{1,0:T(8,128)(2,1)}) %all-gather.3.cloned.1.call-update) | async-done | bytes 5308432 | tf_op jit(solution)/shard_map/all_gather | solution.py:21
  158.7 0.0 slice-start.1
  158.7 4.0 %fusion.15 = bf16[128,1152]{1,0:T(8,128)(2,1)S(1)} fusion(f32[128,1152]{1,0:T(8,128)S(1)} %get-tuple-element.158, bf16[128,2304]{0,1:T(8,128)(2,1)S(1)} %multiply_convert_fusion, bf16[2304,1152]{1,0:T(8,128)(2,1)} %all-gather.3.cloned.1.call-done, bf16[128,1152]{1,0:T(8,128)(2,1)} %param.8), kind=kOutput, calls=%fused_computation.26 | convolution fusion | flops 682721280 | bytes 7077888 | tf_op jit(solution)/shard_map/dot_general | solution.py:24
  162.7 0.0 slice-done
  162.7 0.0 slice-done.1
  162.7 0.0 copy-start.1
  162.7 1.6 fusion.23
  164.3 0.9 copy-done.1
  165.2 1.6 fusion.7
  166.8 1.1 copy.14
  167.9 0.0 reduce-scatter.4.cloned.1.call-update
  167.9 9.3 %all_gather.19 = bf16[256,1152]{1,0:T(8,128)(2,1)} all-gather(bf16[128,1152]{1,0:T(8,128)(2,1)S(1)} %get-tuple-element.157), channel_id=1, replica_groups=mesh['dp'=2,'tp'=4,'section'=4] {'dp'}, dimensions={0}, use_global_device_ids=true | all-gather | bytes 884736 | tf_op jit(solution)/shard_map/all_gather | solution.py:55
  177.2 8.5 %all_gather.18 = bf16[256,1152]{1,0:T(8,128)(2,1)} all-gather(bf16[128,1152]{1,0:T(8,128)(2,1)S(1)} %fusion.15), channel_id=1, replica_groups=mesh['dp'=2,'tp'=4,'section'=4] {'dp'}, dimensions={0}, use_global_device_ids=true | all-gather | bytes 884736 | tf_op jit(solution)/shard_map/all_gather | solution.py:54
  185.7 0.0 all-to-all-done
  185.7 27.0 %while.16 = (s32[]{:T(128)}, f32[1152,1152]{1,0:T(8,128)}, f32[1152,1152]{1,0:T(8,128)}, bf16[256,1152]{1,0:T(8,128)(2,1)S(1)}, bf16[256,1152]{1,0:T(8,128)(2,1)...) while((s32[]{:T(128)}, f32[1152,1152]{1,0:T(8,128)}, ...), condition=%wide.region_7.0_spmd.clone, body=%wide.region_6.0_spmd.clone.sunk | while | flops 690094080 | bytes 33032356 | solution.py:77
  185.7 1.8 convolution_convert_fusion.4
  187.6 3.4 %convolution_convert_fusion.5 = bf16[1152,1152]{1,0:T(8,128)(2,1)} fusion(bf16[256,1152]{1,0:T(8,128)(2,1)} %get-tuple-element.224, s32[]{:T(128)S(6)} %select_n.16, bf16[256,1152]{1,0:T(8,128)(2,1)S(1)} %get-tuple-element.223), kind=kOutput, calls=%fused_computation.1.clone.1 | convolution fusion | flops 341065728 | bytes 3245056 | tf_op jit(solution)/shard_map/while/body/eval_jaxpr/dot_general | solution.py:63
  190.9 6.7 %select_add_fusion.3 = (f32[1152,1152]{1,0:T(8,128)}, f32[1152,1152]{1,0:T(8,128)}) fusion(f32[1152,1152]{1,0:T(8,128)} %get-tuple-element.212, bf16[1152,1152]{1,0:T(8,128)(2,1)S(1)} %convolution_convert_fusion.4, pred[]{:T(512)S(6)} %compare.3, bf16[1152,1152]{1,0:T(8,128)(2,1)} %convolution_convert_fusion.5, f32[1152,1152]{1,0:T(8,128)} %get-tuple-element.211), kind=kLoop, calls=%fused_computation.2.clone.1 | loop fusion | flops 7962624 | bytes 26542080 | tf_op jit(solution)/shard_map/while/body/eval_jaxpr/add | solution.py:72
  197.6 1.8 convolution_convert_fusion.4
  199.5 3.4 %convolution_convert_fusion.5 = bf16[1152,1152]{1,0:T(8,128)(2,1)} fusion(bf16[256,1152]{1,0:T(8,128)(2,1)} %get-tuple-element.224, s32[]{:T(128)S(6)} %select_n.16, bf16[256,1152]{1,0:T(8,128)(2,1)S(1)} %get-tuple-element.223), kind=kOutput, calls=%fused_computation.1.clone.1 | convolution fusion | flops 341065728 | bytes 3245056 | tf_op jit(solution)/shard_map/while/body/eval_jaxpr/dot_general | solution.py:63
  202.8 9.9 %select_add_fusion.3 = (f32[1152,1152]{1,0:T(8,128)}, f32[1152,1152]{1,0:T(8,128)}) fusion(f32[1152,1152]{1,0:T(8,128)} %get-tuple-element.212, bf16[1152,1152]{1,0:T(8,128)(2,1)S(1)} %convolution_convert_fusion.4, pred[]{:T(512)S(6)} %compare.3, bf16[1152,1152]{1,0:T(8,128)(2,1)} %convolution_convert_fusion.5, f32[1152,1152]{1,0:T(8,128)} %get-tuple-element.211), kind=kLoop, calls=%fused_computation.2.clone.1 | loop fusion | flops 7962624 | bytes 26542080 | tf_op jit(solution)/shard_map/while/body/eval_jaxpr/add | solution.py:72
  212.7 0.0 copy-start
  212.7 4.4 %convert_element_type.68 = bf16[1152,1152]{1,0:T(8,128)(2,1)} convert(f32[1152,1152]{1,0:T(8,128)} %get-tuple-element.115) | non-fusion elementwise | flops 1327104 | bytes 7962624 | tf_op jit(solution)/shard_map/convert_element_type | solution.py:84
  217.1 0.2 copy-done
  217.3 1.8 convert_element_type.67
  219.1 3.0 %reduce-scatter.4.cloned.1.call-done = bf16[144,128]{1,0:T(8,128)(2,1)} async-done(((bf16[2304,128]{1,0:T(8,128)(2,1)}), bf16[144,128]{1,0:T(8,128)(2,1)}) %reduce-scatter.4.cloned.1.call-update) | async-done | bytes 36880 | tf_op jit(solution)/shard_map/reduce_scatter | solution.py:35
  222.1 1.1 fusion.20
  223.2 5.5 %psum.15 = f32[144]{0:T(256)} all-reduce(f32[144]{0:T(256)S(1)} %get-tuple-element.141), channel_id=1, replica_groups=mesh['dp'=2,'tp'=4,'section'=4] {'dp'}, use_global_device_ids=true, to_apply=%region_5.0 | all-reduce | flops 144 | bytes 1152 | tf_op jit(solution)/shard_map/psum | solution.py:44
  228.6 29.5 %psum.14 = f32[128]{0:T(128)S(1)} all-reduce(f32[128]{0:T(128)S(1)} %get-tuple-element.142), channel_id=1, replica_groups=mesh['dp'=2,'tp'=4,'section'=4] {'tp','section'}, use_global_device_ids=true, to_apply=%region_3.0 | all-reduce | flops 128 | bytes 1024 | tf_op jit(solution)/shard_map/psum | solution.py:45
  258.1 1.6 fusion.17
  (5 shorter events, 0.0 us)
Async XLA Ops:
  7.2 1.5 copy-start.3
  7.2 10.9 %copy-start.4 = (f32[2304]{0:T(1024)S(1)}, f32[2304]{0:T(1024)}, u32[]{:S(2)}) copy-start(f32[2304]{0:T(1024)} %param.9) | copy-start | bytes 27652
  7.2 80.7 %all-gather.5.cloned.1.call-start = ((), (), s32[]{:S(2)}) async-start(), calls=%async_computation.3 | async-start | bytes 7962624 | tf_op jit(solution)/shard_map/all_gather | solution.py:20
  7.9 80.0 %copy-start.2 = (bf16[128,1152]{1,0:T(8,128)(2,1)S(1)}, bf16[128,1152]{1,0:T(8,128)(2,1)}, u32[]{:S(2)}) copy-start(bf16[128,1152]{1,0:T(8,128)(2,1)} %param.8) | copy-start | bytes 884740
  7.9 150.8 %all-gather.3.cloned.1.call-start = ((), (), s32[]{:S(2)}) async-start(), calls=%async_computation.2 | async-start | bytes 7962624 | tf_op jit(solution)/shard_map/all_gather | solution.py:21
  19.5 166.2 %all-to-all-start = ((bf16[128,2,1152]{2,0,1:T(8,128)(2,1)}), bf16[128,2,1152]{2,0,1:T(8,128)(2,1)S(1)}, u32[]{:S(2)}, u32[]{:S(2)}) async-start(bf16[128,2,1152]{2,0,1:T(8,128)(2,1)} %copy.13), calls=%async_computation | async-start | bytes 1179648 | tf_op jit(solution)/shard_map/all_to_all | solution.py:51
  23.0 199.1 %reduce-scatter.4.cloned.1.call-start = ((), (), s32[]{:S(2)}) async-start(), calls=%async_computation.4 | async-start | bytes 626688 | tf_op jit(solution)/shard_map/reduce_scatter | solution.py:35
  87.9 74.8 %slice-start = ((s8[5308416]{0:T(1024)(128)(4,1)}), s8[1114112]{0:T(1024)(128)(4,1)S(1)}, s32[]{:S(2)}) async-start(s8[5308416]{0:T(1024)(128)(4,1)} %bitcast.30), calls=%async_computation.5 | async-start | bytes 2228224
  158.7 4.0 %slice-start.1 = ((s8[5308416]{0:T(1024)(128)(4,1)}), s8[4194304]{0:T(1024)(128)(4,1)S(1)}, s32[]{:S(2)}) async-start(s8[5308416]{0:T(1024)(128)(4,1)} %bitcast.30), calls=%async_computation.6 | async-start | bytes 8388608
  162.7 2.5 copy-start.1
  212.7 4.7 %copy-start = (f32[1152,1152]{1,0:T(8,128)S(1)}, f32[1152,1152]{1,0:T(8,128)}, u32[]{:S(2)}) copy-start(f32[1152,1152]{1,0:T(8,128)} %get-tuple-element.114) | copy-start | bytes 15925252
Sparse Core Ops, SparseCore 0:
  9.5 78.3 all-gather.4
  89.4 69.2 all-gather.2
  168.0 54.0 reduce-scatter.3
where the time goes:
time: 267 us; the launch traced here: 266 us
  waiting for transfers between devices  135 us (51%)
  blocking collectives  61.8 us (23%)
  other arithmetic  27.3 us (10%)
  matrix products  21.2 us (8%)
  between operations  13.9 us (5%)
  starting transfers between devices  3.64 us (1%)
  local copies, waits for them, and re-layouts  3.38 us (1%)
    all_gather x1, waiting for transfers between devices, shards(): lax.all_gather(w_up, 'dp', axis=0, tiled=True)  67.1 us
    all_gather x1, waiting for transfers between devices, shards(): lax.all_gather(w_gate, 'dp', axis=0, tiled=True)  63.6 us
    psum x1, blocking collectives, shards(): row_sum = lax.psum(row_part, ('tp', 'section'))  29.5 us
    add x2, other arithmetic, one_block(): total + lax.optimization_barrier(term.astype(jnp.bfloat16)).astype(jnp.fl...  16.6 us
    all_gather x1, blocking collectives, shards(): piece_up = lax.all_gather(d_up, 'dp', axis=0, tiled=True)  9.34 us
    all_gather x1, blocking collectives, shards(): rows_in = lax.all_gather(tokens, 'section', axis=1, tiled=True)  9.03 us
    all_gather x1, blocking collectives, shards(): piece_gate = lax.all_gather(d_gate, 'dp', axis=0, tiled=True)  8.47 us
    dot_general x2, matrix products, one_block(): lax.dot_general(block_normed, block_gate, contract_rows, preferred_elemen...  6.71 us
  transfers between devices with their start and end apart: 4, of which 3 were waited for; matrix products, arithmetic and copies ran while one was open for 18% of the time, Pallas kernels for 0%

commit v1 on v0

--- a/solution.py
+++ b/solution.py
@@ -5,6 +5,12 @@
 
 D = 2304
 epsilon = 1e-06
+
+
+def gather_pair(value, axis, along):
+    theirs = lax.ppermute(value, axis, [(0, 1), (1, 0)])
+    row_of_blocks = jnp.concatenate([value, theirs], axis=along)
+    return jnp.roll(row_of_blocks, lax.axis_index(axis) * value.shape[along], axis=along)
 
 
 def gated_unit(gate, up):
@@ -17,7 +23,7 @@
     inv_rms = lax.rsqrt(jnp.mean(inputs * inputs, axis=1) + epsilon)
     normed = (inputs * inv_rms[:, None] * norm_gain).astype(jnp.bfloat16)
     full_gate, full_up = (
-        lax.all_gather(w_gate, "dp", axis=0, tiled=True),
+        gather_pair(w_gate, "dp", 0),
         lax.all_gather(w_up, "dp", axis=0, tiled=True),
     )
     gate = jnp.dot(normed, full_gate, preferred_element_type=jnp.float32)

time: 267 us -> 268 us (level)
  other arithmetic: 27.3 us -> 39.4 us
  waiting for transfers between devices: 135 us -> 124 us
  blocking collectives: 61.8 us -> 58.4 us
  starting transfers between devices: 3.64 us -> 6.63 us
    all_to_all x1, waiting for transfers between devices: 0.01 us -> 101 us  [shards(): lax.all_to_all(normed, 'dp', split_axis=1, concat_axis=0, tiled=True)]
    all_gather x1, waiting for transfers between devices: 67.1 us -> 0.01 us  [shards(): lax.all_gather(w_up, 'dp', axis=0, tiled=True)]
    all_gather x1 -> x0, waiting for transfers between devices: 63.6 us -> none  [shards(): lax.all_gather(w_gate, 'dp', axis=0, tiled=True)]
    reduce_scatter x1, waiting for transfers between devices: 2.99 us -> 22.6 us  [shards(): lax.psum_scatter((first + second).astype(jnp.bfloat16), ('tp', 'section')...]
    concatenate x0 -> x1, other arithmetic: none -> 10.5 us  [gather_pair(): jnp.roll(row_of_blocks, lax.axis_index(axis) * value.shape[along], axis=a...]
    ppermute x0 -> x1, starting transfers between devices: none -> 3.03 us  [gather_pair(): theirs = lax.ppermute(value, axis, [(0, 1), (1, 0)])]
  transfers between devices with their start and end apart: 4 -> 4, of which waited for: 3 -> 2; matrix products, arithmetic and copies ran while one was open for 18% -> 19% of each run, Pallas kernels for 0% -> 0%
where the time goes in v1:
time: 268 us; the launch traced here: 267 us
  waiting for transfers between devices  124 us (46%)
  blocking collectives  58.4 us (22%)
  other arithmetic  39.4 us (15%)
  matrix products  20.7 us (8%)
  between operations  14.2 us (5%)
  starting transfers between devices  6.63 us (2%)
  local copies, waits for them, and re-layouts  3.52 us (1%)
    all_to_all x1, waiting for transfers between devices, shards(): lax.all_to_all(normed, 'dp', split_axis=1, concat_axis=0, tiled=True)  101 us
    psum x1, blocking collectives, shards(): row_sum = lax.psum(row_part, ('tp', 'section'))  29.5 us
    reduce_scatter x1, waiting for transfers between devices, shards(): lax.psum_scatter((first + second).astype(jnp.bfloat16), ('tp', 'section')...  22.6 us
    add x2, other arithmetic, one_block(): total + lax.optimization_barrier(term.astype(jnp.bfloat16)).astype(jnp.fl...  16.7 us
    concatenate x1, other arithmetic, gather_pair(): jnp.roll(row_of_blocks, lax.axis_index(axis) * value.shape[along], axis=a...  10.5 us
    all_gather x1, blocking collectives, shards(): piece_up = lax.all_gather(d_up, 'dp', axis=0, tiled=True)  7.84 us
    all_gather x1, blocking collectives, shards(): piece_gate = lax.all_gather(d_gate, 'dp', axis=0, tiled=True)  7.81 us
    all_gather x1, blocking collectives, shards(): rows_in = lax.all_gather(tokens, 'section', axis=1, tiled=True)  7.75 us
  transfers between devices with their start and end apart: 4, of which 2 were waited for; matrix products, arithmetic and copies ran while one was open for 19% of the time, Pallas kernels for 0%

profile of v1, /device:TPU:0, one launch (start us, length us, event | category | flops | bytes accessed | tf_op | source)
XLA Modules:
  0.0 267.2 jit_solution(6971587140816017058)
XLA Ops:
  7.2 0.0 all-gather.2.cloned.1.call-start
  7.2 0.7 all-gather.2.cloned.1.call-update
  7.9 3.0 %collective-permute-start = (bf16[1152,1152]{1,0:T(8,128)(2,1)}, bf16[1152,1152]{1,0:T(8,128)(2,1)}, u32[]{:S(2)}, u32[]{:S(2)}) collective-permute-start(bf16[1152,1152]{1,0:T(8,128)(2,1)} %param.10), channel_id=1, source_target_pairs={{0,16},{16,0},{1,17},{17,1},{2,18},{18,2},{3,19},{19,3},{4,20},{20... | collective-permute-start | bytes 7962632 | tf_op jit(solution)/shard_map/ppermute | solution.py:11
  10.9 7.8 %all_gather.12 = bf16[128,2304]{0,1:T(8,128)(2,1)S(1)} all-gather(bf16[128,576]{0,1:T(8,128)(2,1)} %param.7), channel_id=1, replica_groups=mesh['dp'=2,'tp'=4,'section'=4] {'section'}, dimensions={1}, use_global_device_ids=true | all-gather | bytes 737280 | tf_op jit(solution)/shard_map/all_gather | solution.py:21
  18.7 0.3 multiply_reduce_fusion
  19.0 1.9 multiply_convert_fusion
  20.9 3.5 %all-to-all-start = ((bf16[128,2,1152]{0,2,1:T(8,128)(2,1)}), bf16[128,2,1152]{0,2,1:T(8,128)(2,1)S(1)}, u32[]{:S(2)}, u32[]{:S(2)}) async-start(bf16[128,2,1152]{0,2,1:T(8,128)(2,1)} %bitcast.2), calls=%async_computation.1 | async-start | bytes 1179648 | tf_op jit(solution)/shard_map/all_to_all | solution.py:57
  24.4 0.0 reduce-scatter.2.cloned.1.call-start
  24.5 1.1 convert_element_type.56
  25.6 0.8 dynamic_slice.31
  26.4 101.1 %all-to-all-done = bf16[128,2,1152]{0,2,1:T(8,128)(2,1)S(1)} async-done(((bf16[128,2,1152]{0,2,1:T(8,128)(2,1)}), bf16[128,2,1152]{0,2,1:T(8,128)(2,1)S(1)}, u32[]{:S(2)}, u32[]{:S(2)}) %all-to-all-start) | async-done | bytes 589856 | tf_op jit(solution)/shard_map/all_to_all | solution.py:57
  127.5 0.3 copy.10
  127.8 0.0 copy-start.3
  127.8 0.0 collective-permute-done
  127.9 10.5 %fusion.8 = bf16[2304,1152]{1,0:T(8,128)(2,1)S(1)} fusion(s32[]{:T(128)S(6)} %select_n.28, bf16[1152,1152]{1,0:T(8,128)(2,1)} %param.10, bf16[1152,1152]{1,0:T(8,128)(2,1)} %collective-permute-done), kind=kLoop, calls=%fused_computation.16 | loop fusion | flops 21233664 | bytes 10616836 | tf_op jit(solution)/shard_map/jit(_roll_dynamic)/concatenate | solution.py:13
  138.3 0.0 copy-start.2
  138.3 2.3 copy-done.2
  140.6 0.0 copy-done.3
  140.6 2.2 fusion.10
  142.8 7.8 %all_gather.15 = bf16[256,1152]{1,0:T(8,128)(2,1)} all-gather(bf16[128,1152]{1,0:T(8,128)(2,1)S(1)} %get-tuple-element.153), channel_id=1, replica_groups=mesh['dp'=2,'tp'=4,'section'=4] {'dp'}, dimensions={0}, use_global_device_ids=true | all-gather | bytes 884736 | tf_op jit(solution)/shard_map/all_gather | solution.py:61
  150.7 0.0 all-gather.2.cloned.1.call-done
  150.7 0.0 copy-start.1
  150.7 4.1 %fusion.17 = bf16[128,1152]{1,0:T(8,128)(2,1)S(1)} fusion(f32[128,1152]{1,0:T(8,128)S(1)} %get-tuple-element.154, bf16[128,2304]{0,1:T(8,128)(2,1)} %multiply_convert_fusion, bf16[2304,1152]{1,0:T(8,128)(2,1)} %all-gather.2.cloned.1.call-done, bf16[128,1152]{1,0:T(8,128)(2,1)S(1)} %copy-done.3), kind=kOutput, calls=%fused_computation.33 | convolution fusion | flops 682721280 | bytes 7077888 | tf_op jit(solution)/shard_map/dot_general | solution.py:30
  154.8 0.0 slice-start
  154.8 7.8 %all_gather.14 = bf16[256,1152]{1,0:T(8,128)(2,1)} all-gather(bf16[128,1152]{1,0:T(8,128)(2,1)S(1)} %fusion.17), channel_id=1, replica_groups=mesh['dp'=2,'tp'=4,'section'=4] {'dp'}, dimensions={0}, use_global_device_ids=true | all-gather | bytes 884736 | tf_op jit(solution)/shard_map/all_gather | solution.py:60
  162.6 0.0 copy-done.1
  162.6 0.0 slice-start.1
  162.6 1.6 convolution_bitcast_fusion
  164.2 0.0 slice-done
  164.2 0.0 slice-done.1
  164.2 2.4 fusion.9
  166.6 0.0 reduce-scatter.2.cloned.1.call-update
  166.6 27.2 %while.16 = (s32[]{:T(128)}, f32[1152,1152]{1,0:T(8,128)}, f32[1152,1152]{1,0:T(8,128)}, bf16[256,1152]{1,0:T(8,128)(2,1)S(1)}, bf16[256,1152]{1,0:T(8,128)(2,1)...) while((s32[]{:T(128)}, f32[1152,1152]{1,0:T(8,128)}, ...), condition=%wide.region_7.8_spmd.clone, body=%wide.region_6.7_spmd.clone.sunk | while | flops 690094080 | bytes 33032356 | solution.py:83
  166.6 1.9 convolution_convert_fusion.4
  168.5 3.4 %convolution_convert_fusion.5 = bf16[1152,1152]{1,0:T(8,128)(2,1)} fusion(bf16[256,1152]{1,0:T(8,128)(2,1)} %get-tuple-element.220, s32[]{:T(128)S(6)} %select_n.31, bf16[256,1152]{1,0:T(8,128)(2,1)S(1)} %get-tuple-element.219), kind=kOutput, calls=%fused_computation.1.clone.1 | convolution fusion | flops 341065728 | bytes 3245056 | tf_op jit(solution)/shard_map/while/body/eval_jaxpr/dot_general | solution.py:69
  171.8 6.8 %select_add_fusion.3 = (f32[1152,1152]{1,0:T(8,128)}, f32[1152,1152]{1,0:T(8,128)}) fusion(f32[1152,1152]{1,0:T(8,128)} %get-tuple-element.208, bf16[1152,1152]{1,0:T(8,128)(2,1)S(1)} %convolution_convert_fusion.4, pred[]{:T(512)S(6)} %compare.3, bf16[1152,1152]{1,0:T(8,128)(2,1)} %convolution_convert_fusion.5, f32[1152,1152]{1,0:T(8,128)} %get-tuple-element.207), kind=kLoop, calls=%fused_computation.2.clone.1 | loop fusion | flops 7962624 | bytes 26542080 | tf_op jit(solution)/shard_map/while/body/eval_jaxpr/add | solution.py:78
  178.7 1.8 convolution_convert_fusion.4
  180.5 3.4 %convolution_convert_fusion.5 = bf16[1152,1152]{1,0:T(8,128)(2,1)} fusion(bf16[256,1152]{1,0:T(8,128)(2,1)} %get-tuple-element.220, s32[]{:T(128)S(6)} %select_n.31, bf16[256,1152]{1,0:T(8,128)(2,1)S(1)} %get-tuple-element.219), kind=kOutput, calls=%fused_computation.1.clone.1 | convolution fusion | flops 341065728 | bytes 3245056 | tf_op jit(solution)/shard_map/while/body/eval_jaxpr/dot_general | solution.py:69
  183.9 9.9 %select_add_fusion.3 = (f32[1152,1152]{1,0:T(8,128)}, f32[1152,1152]{1,0:T(8,128)}) fusion(f32[1152,1152]{1,0:T(8,128)} %get-tuple-element.208, bf16[1152,1152]{1,0:T(8,128)(2,1)S(1)} %convolution_convert_fusion.4, pred[]{:T(512)S(6)} %compare.3, bf16[1152,1152]{1,0:T(8,128)(2,1)} %convolution_convert_fusion.5, f32[1152,1152]{1,0:T(8,128)} %get-tuple-element.207), kind=kLoop, calls=%fused_computation.2.clone.1 | loop fusion | flops 7962624 | bytes 26542080 | tf_op jit(solution)/shard_map/while/body/eval_jaxpr/add | solution.py:78
  193.8 0.0 copy-start
  193.8 4.4 %convert_element_type.64 = bf16[1152,1152]{1,0:T(8,128)(2,1)} convert(f32[1152,1152]{1,0:T(8,128)} %get-tuple-element.115) | non-fusion elementwise | flops 1327104 | bytes 7962624 | tf_op jit(solution)/shard_map/convert_element_type | solution.py:90
  198.2 0.1 copy-done
  198.4 1.8 convert_element_type.63
  200.1 22.6 %reduce-scatter.2.cloned.1.call-done = bf16[144,128]{1,0:T(8,128)(2,1)} async-done(((bf16[2304,128]{1,0:T(8,128)(2,1)}), bf16[144,128]{1,0:T(8,128)(2,1)}) %reduce-scatter.2.cloned.1.call-update) | async-done | bytes 36880 | tf_op jit(solution)/shard_map/reduce_scatter | solution.py:41
  222.8 1.1 fusion.22
  223.8 5.5 %psum.15 = f32[144]{0:T(256)} all-reduce(f32[144]{0:T(256)S(1)} %get-tuple-element.137), channel_id=1, replica_groups=mesh['dp'=2,'tp'=4,'section'=4] {'dp'}, use_global_device_ids=true, to_apply=%region_5.6 | all-reduce | flops 144 | bytes 1152 | tf_op jit(solution)/shard_map/psum | solution.py:50
  229.3 29.5 %psum.14 = f32[128]{0:T(128)S(1)} all-reduce(f32[128]{0:T(128)S(1)} %get-tuple-element.138), channel_id=1, replica_groups=mesh['dp'=2,'tp'=4,'section'=4] {'tp','section'}, use_global_device_ids=true, to_apply=%region_3.4 | all-reduce | flops 128 | bytes 1024 | tf_op jit(solution)/shard_map/psum | solution.py:51
  258.8 1.6 fusion.19
  (5 shorter events, 0.0 us)
Async XLA Ops:
  7.2 143.5 %all-gather.2.cloned.1.call-start = ((), (), s32[]{:S(2)}) async-start(), calls=%async_computation.2 | async-start | bytes 7962624 | tf_op jit(solution)/shard_map/all_gather | solution.py:27
  7.9 119.9 %collective-permute-start = (bf16[1152,1152]{1,0:T(8,128)(2,1)}, bf16[1152,1152]{1,0:T(8,128)(2,1)}, u32[]{:S(2)}, u32[]{:S(2)}) collective-permute-start(bf16[1152,1152]{1,0:T(8,128)(2,1)} %param.10), channel_id=1, source_target_pairs={{0,16},{16,0},{1,17},{17,1},{2,18},{18,2},{3,19},{19,3},{4,20},{20... | collective-permute-start | bytes 7962632 | tf_op jit(solution)/shard_map/ppermute | solution.py:11
  20.9 106.6 %all-to-all-start = ((bf16[128,2,1152]{0,2,1:T(8,128)(2,1)}), bf16[128,2,1152]{0,2,1:T(8,128)(2,1)S(1)}, u32[]{:S(2)}, u32[]{:S(2)}) async-start(bf16[128,2,1152]{0,2,1:T(8,128)(2,1)} %bitcast.2), calls=%async_computation.1 | async-start | bytes 1179648 | tf_op jit(solution)/shard_map/all_to_all | solution.py:57
  24.4 198.3 %reduce-scatter.2.cloned.1.call-start = ((), (), s32[]{:S(2)}) async-start(), calls=%async_computation.3 | async-start | bytes 626688 | tf_op jit(solution)/shard_map/reduce_scatter | solution.py:41
  127.8 12.8 %copy-start.3 = (bf16[128,1152]{1,0:T(8,128)(2,1)S(1)}, bf16[128,1152]{1,0:T(8,128)(2,1)}, u32[]{:S(2)}) copy-start(bf16[128,1152]{1,0:T(8,128)(2,1)} %param.8) | copy-start | bytes 884740
  138.3 2.3 copy-start.2
  150.7 11.9 %copy-start.1 = (bf16[2304,1152]{1,0:T(8,128)(2,1)S(1)}, bf16[2304,1152]{1,0:T(8,128)(2,1)}, u32[]{:S(2)}) copy-start(bf16[2304,1152]{1,0:T(8,128)(2,1)} %all-gather.2.cloned.1.call-done) | copy-start | bytes 15925252
  154.8 9.4 %slice-start = ((s8[5308416]{0:T(1024)(128)(4,1)}), s8[4194304]{0:T(1024)(128)(4,1)S(1)}, s32[]{:S(2)}) async-start(s8[5308416]{0:T(1024)(128)(4,1)} %bitcast.27), calls=%async_computation.4 | async-start | bytes 8388608
  162.6 1.6 slice-start.1
  193.8 4.6 %copy-start = (f32[1152,1152]{1,0:T(8,128)S(1)}, f32[1152,1152]{1,0:T(8,128)}, u32[]{:S(2)}) copy-start(f32[1152,1152]{1,0:T(8,128)} %get-tuple-element.114) | copy-start | bytes 15925252
Sparse Core Ops, SparseCore 0:
  9.5 122.6 all-gather.1
  166.7 55.9 reduce-scatter.1
